TPU v7x, 32 devices: a whole 2x2x4 slice. The times are simulated.
32 devices in a mesh: gx: 4 (over z), gy: 8 (over y, x, core).
Axes of the slice: x: 2, y: 2, z: 4, core: 2. Of those that a mesh axis runs over, the one named last changes fastest.
Arguments:
- node_coords: float32 [12288, 3, 128], P(('gx', 'gy')), may hold values from -6 to 6
- node_disp: float32 [12288, 3, 128], P(('gx', 'gy')), may hold values from -6 to 6
- qpoints: float32 [8192, 3, 256], P(('gx', 'gy')), may hold values from -6 to 6
- qweights: float32 [8192, 256], P(('gx', 'gy')), may hold values from 0.1 to 2
- qcount: int32 [8192], P(('gx', 'gy')), may hold values from 64 to 256
- sec_block: int32 [8192], P(('gx', 'gy')), may hold values from 0 to 12287, as said below
- pri_block: int32 [8192], P(('gx', 'gy')), may hold values from 0 to 12287, as said below
Outputs:
- gap: float32 [12288, 3, 128], P(('gx', 'gy'))
Inputs may be any that keep to these rules, and one draw needn't show every extreme that they name: `sec_block`: patch b is owned by device b // 384. Among the segments of one device, at most 16 have their secondary patch owned by any one device; in every draw some device owns the secondary patches of exactly 16 segments of every device. `pri_block`: as for sec_block, with primary patches: at most 16 segments of one device name patches of any one owner, and some owner gets exactly 16 from every device.
All inputs are finite; a program needn't handle non-finite values.
Results may differ from a plain program's by a relative error of at most 0.000098.
Values sent between devices are 32-bit elements; how exact they have to be, the bound alone decides.
A program may use at most 64 MiB of HBM per device.

v0:
```python
import jax
import jax.numpy as jnp
from jax import lax
from jax.sharding import PartitionSpec as P


def shape_values(points, coords):
    diff0 = points[:, 0, :, None] - coords[:, 0, None, :]
    diff1 = points[:, 1, :, None] - coords[:, 1, None, :]
    diff2 = points[:, 2, :, None] - coords[:, 2, None, :]
    radius = diff0 * diff0 + diff1 * diff1 + diff2 * diff2
    kernel = 1.0 / (1.0 + 2.0 * radius)
    return kernel / jnp.sum(kernel, axis=-1, keepdims=True)


def routing(block_ids, blocks_dev, capacity, slot_count):
    owners = block_ids // blocks_dev
    local_ids = block_ids % blocks_dev
    positions = jnp.arange(block_ids.shape[0], dtype=jnp.int32)
    same_owner = (owners[:, None] == owners[None, :]) & (positions[:, None] > positions[None, :])
    ranks = jnp.sum(same_owner.astype(jnp.int32), axis=1)
    slot_ids = owners * capacity + ranks
    matches = slot_ids[:, None] == jnp.arange(slot_count, dtype=jnp.int32)[None, :]
    request = jnp.sum(jnp.where(matches, local_ids[:, None], 0), axis=0)
    return (slot_ids, matches, request)


def body(node_coords, node_disp, qpoints, qweights, qcount, sec_block, pri_block):
    grid_x = lax.axis_size("gx")
    grid_y = lax.axis_size("gy")
    devices = grid_x * grid_y
    blocks_dev = node_coords.shape[0]
    node_count = node_coords.shape[2]
    seg_count = qpoints.shape[0]
    quad_points = qpoints.shape[2]
    slot_count = 2 * seg_count
    capacity = slot_count // devices
    hp = lax.Precision.HIGHEST
    sec_slots, sec_matches, sec_request = routing(sec_block, blocks_dev, capacity, slot_count)
    pri_slots, pri_matches, pri_request = routing(pri_block, blocks_dev, capacity, slot_count)
    requests = jnp.stack([sec_request, pri_request], axis=-1)
    received = lax.all_to_all(
        requests.reshape(devices, capacity, 2),
        ("gx", "gy"),
        split_axis=0,
        concat_axis=0,
        tiled=True,
    )
    received = received.reshape(slot_count, 2)
    node_data = jnp.concatenate([node_coords, node_disp], axis=1)
    outgoing = jnp.stack(
        [jnp.take(node_data, received[:, 0], axis=0), jnp.take(node_data, received[:, 1], axis=0)],
        axis=1,
    )
    fetched = lax.all_to_all(
        outgoing.reshape(devices, capacity, 2, 6, node_count),
        ("gx", "gy"),
        split_axis=0,
        concat_axis=0,
        tiled=True,
    )
    fetched = fetched.reshape(slot_count, 2, 6, node_count)
    sec_nodes = jnp.take(fetched[:, 0], sec_slots, axis=0)
    pri_nodes = jnp.take(fetched[:, 1], pri_slots, axis=0)
    live = jnp.arange(quad_points, dtype=jnp.int32)[None, :] < qcount[:, None]
    weights = jnp.where(live, qweights, jnp.zeros_like(qweights))
    seg_group = 16
    groups = seg_count // seg_group

    def one_group(inputs):
        points, quad_weights, sec_here, pri_here = inputs
        sec_shape = shape_values(points, sec_here[:, :3])
        pri_shape = shape_values(points, pri_here[:, :3])
        weighted = quad_weights[:, :, None] * sec_shape
        dense_sec = jnp.einsum("gqk,gqj->gkj", weighted, sec_shape, precision=hp)
        dense_mix = jnp.einsum("gqk,gqj->gkj", weighted, pri_shape, precision=hp)
        return jnp.einsum("gkj,gcj->gck", dense_sec, sec_here[:, 3:], precision=hp) - jnp.einsum(
            "gkj,gcj->gck", dense_mix, pri_here[:, 3:], precision=hp
        )

    contrib = lax.map(
        one_group,
        (
            qpoints.reshape(groups, seg_group, 3, quad_points),
            weights.reshape(groups, seg_group, quad_points),
            sec_nodes.reshape(groups, seg_group, 6, node_count),
            pri_nodes.reshape(groups, seg_group, 6, node_count),
        ),
    )
    contrib = contrib.reshape(seg_count, 3, node_count)
    placing = sec_matches.astype(jnp.float32)
    parcels = jnp.einsum("sp,scn->pcn", placing, contrib, precision=hp)
    incoming = lax.all_to_all(
        parcels.reshape(devices, capacity, 3, node_count),
        ("gx", "gy"),
        split_axis=0,
        concat_axis=0,
        tiled=True,
    )
    incoming = incoming.reshape(slot_count, 3, node_count)
    select = (jnp.arange(blocks_dev, dtype=jnp.int32)[:, None] == received[None, :, 0]).astype(
        jnp.float32
    )
    return jnp.einsum("bp,pcn->bcn", select, incoming, precision=hp)


def solution(mesh):
    placed = (
        P(("gx", "gy"), None, None),
        P(("gx", "gy"), None, None),
        P(("gx", "gy"), None, None),
        P(("gx", "gy"), None),
        P(("gx", "gy")),
        P(("gx", "gy")),
        P(("gx", "gy")),
    )
    return jax.shard_map(
        body, mesh=mesh, in_specs=placed, out_specs=P(("gx", "gy"), None, None), check_vma=False
    )
```

profile of v0, /device:TPU:0, one launch (start us, length us, event | category | flops | bytes accessed | tf_op | source)
XLA Modules:
  0.0 436.3 jit_solution(3195656575965883801)
XLA Ops:
  2.9 7.3 %all-to-all-start = ((s32[32,16,2]{1,2,0:T(2,128)}), s32[32,16,2]{1,2,0:T(2,128)S(1)}, u32[]{:S(2)}, u32[]{:S(2)}) async-start(s32[32,16,2]{1,2,0:T(2,128)} %copy.42), calls=%async_computation | async-start | bytes 65536 | tf_op jit(solution)/shard_map/all_to_all | solution.py:42
  36.8 70.2 %all-to-all-done.1 = f32[32,16,2,6,128]{4,1,3,2,0:T(8,128)S(1)} async-done(((f32[32,16,2,6,128]{4,1,3,2,0:T(8,128)}), f32[32,16,2,6,128]{4,1,3,2,0:T(8,128)S(1)}, u32[]{:S(2)}, u32[]{:S(2)}) %all-to-all-start.1) | async-done | bytes 3145760 | tf_op jit(solution)/shard_map/all_to_all | solution.py:55
  115.8 293.9 %while.10 = (s32[]{:T(128)}, f32[16,16,3,128]{3,2,1,0:T(4,128)S(1)}, f32[16,16,6,128]{3,2,1,0:T(8,128)}, f32[16,16,256]{2,1,0:T(8,128)S(1)}, f32[16,16,3,256]{3,...) while((s32[]{:T(128)}, f32[16,16,3,128]{3,2,1,0:T(4,128)S(1)}, f32[16,16,6,128]{3,2,1,0:T(8,128)}, ...), condition=%wide.region_7.10_spmd, body=%wide.region_4.9_spmd.sunk | while | flops 1668282368 | bytes 5259357 | solution.py:81
  119.7 5.5 %fusion.70 = f32[16,128,128]{2,1,0:T(8,128)S(1)} fusion(f32[16,256]{1,0:T(8,128)S(1)} %get-tuple-element.157, f32[16,128]{1,0:T(8,128)S(1)} %bitcast.101, f32[16,128]{1,0:T(8,128)S(1)} %bitcast.103, f32[16,128]{1,0:T(8,128)S(1)} %bitcast.99, f32[16,256]{1,0:T(8,128)S(1)} %get-tuple-element.149, f32[16,256]{1,0:T(8,128)S(1)} %get-tuple-element.150, ...), kind=kOutput, calls=%fused_computation.4.clone.1 | convolution fusion | flops 818413568 | bytes 1196032 | tf_op jit(solution)/shard_map/while/body/eval_jaxpr/gqk,gqj->gkj/dot_general | solution.py:76
  138.1 5.5 %fusion.70 = f32[16,128,128]{2,1,0:T(8,128)S(1)} fusion(f32[16,256]{1,0:T(8,128)S(1)} %get-tuple-element.157, f32[16,128]{1,0:T(8,128)S(1)} %bitcast.101, f32[16,128]{1,0:T(8,128)S(1)} %bitcast.103, f32[16,128]{1,0:T(8,128)S(1)} %bitcast.99, f32[16,256]{1,0:T(8,128)S(1)} %get-tuple-element.149, f32[16,256]{1,0:T(8,128)S(1)} %get-tuple-element.150, ...), kind=kOutput, calls=%fused_computation.4.clone.1 | convolution fusion | flops 818413568 | bytes 1196032 | tf_op jit(solution)/shard_map/while/body/eval_jaxpr/gqk,gqj->gkj/dot_general | solution.py:76
  143.6 5.5 %fusion.68 = f32[16,128,128]{2,1,0:T(8,128)S(1)} fusion(f32[16,256]{1,0:T(8,128)S(1)} %get-tuple-element.156, f32[16,128]{1,0:T(8,128)S(1)} %bitcast.94, f32[16,256]{1,0:T(8,128)S(1)} %get-tuple-element.149, f32[16,128]{1,0:T(8,128)S(1)} %bitcast.97, f32[16,256]{1,0:T(8,128)S(1)} %get-tuple-element.150, f32[16,128]{1,0:T(8,128)S(1)} %bitcast.91, ...), kind=kOutput, calls=%fused_computation.6.clone.1 | convolution fusion | flops 818413568 | bytes 1155072 | tf_op jit(solution)/shard_map/while/body/eval_jaxpr/gqk,gqj->gkj/dot_general | solution.py:75
  156.4 5.5 %fusion.70 = f32[16,128,128]{2,1,0:T(8,128)S(1)} fusion(f32[16,256]{1,0:T(8,128)S(1)} %get-tuple-element.157, f32[16,128]{1,0:T(8,128)S(1)} %bitcast.101, f32[16,128]{1,0:T(8,128)S(1)} %bitcast.103, f32[16,128]{1,0:T(8,128)S(1)} %bitcast.99, f32[16,256]{1,0:T(8,128)S(1)} %get-tuple-element.149, f32[16,256]{1,0:T(8,128)S(1)} %get-tuple-element.150, ...), kind=kOutput, calls=%fused_computation.4.clone.1 | convolution fusion | flops 818413568 | bytes 1196032 | tf_op jit(solution)/shard_map/while/body/eval_jaxpr/gqk,gqj->gkj/dot_general | solution.py:76
  161.9 5.5 %fusion.68 = f32[16,128,128]{2,1,0:T(8,128)S(1)} fusion(f32[16,256]{1,0:T(8,128)S(1)} %get-tuple-element.156, f32[16,128]{1,0:T(8,128)S(1)} %bitcast.94, f32[16,256]{1,0:T(8,128)S(1)} %get-tuple-element.149, f32[16,128]{1,0:T(8,128)S(1)} %bitcast.97, f32[16,256]{1,0:T(8,128)S(1)} %get-tuple-element.150, f32[16,128]{1,0:T(8,128)S(1)} %bitcast.91, ...), kind=kOutput, calls=%fused_computation.6.clone.1 | convolution fusion | flops 818413568 | bytes 1155072 | tf_op jit(solution)/shard_map/while/body/eval_jaxpr/gqk,gqj->gkj/dot_general | solution.py:75
  174.8 5.5 %fusion.70 = f32[16,128,128]{2,1,0:T(8,128)S(1)} fusion(f32[16,256]{1,0:T(8,128)S(1)} %get-tuple-element.157, f32[16,128]{1,0:T(8,128)S(1)} %bitcast.101, f32[16,128]{1,0:T(8,128)S(1)} %bitcast.103, f32[16,128]{1,0:T(8,128)S(1)} %bitcast.99, f32[16,256]{1,0:T(8,128)S(1)} %get-tuple-element.149, f32[16,256]{1,0:T(8,128)S(1)} %get-tuple-element.150, ...), kind=kOutput, calls=%fused_computation.4.clone.1 | convolution fusion | flops 818413568 | bytes 1196032 | tf_op jit(solution)/shard_map/while/body/eval_jaxpr/gqk,gqj->gkj/dot_general | solution.py:76
  193.2 5.5 %fusion.70 = f32[16,128,128]{2,1,0:T(8,128)S(1)} fusion(f32[16,256]{1,0:T(8,128)S(1)} %get-tuple-element.157, f32[16,128]{1,0:T(8,128)S(1)} %bitcast.101, f32[16,128]{1,0:T(8,128)S(1)} %bitcast.103, f32[16,128]{1,0:T(8,128)S(1)} %bitcast.99, f32[16,256]{1,0:T(8,128)S(1)} %get-tuple-element.149, f32[16,256]{1,0:T(8,128)S(1)} %get-tuple-element.150, ...), kind=kOutput, calls=%fused_computation.4.clone.1 | convolution fusion | flops 818413568 | bytes 1196032 | tf_op jit(solution)/shard_map/while/body/eval_jaxpr/gqk,gqj->gkj/dot_general | solution.py:76
  211.5 5.5 %fusion.70 = f32[16,128,128]{2,1,0:T(8,128)S(1)} fusion(f32[16,256]{1,0:T(8,128)S(1)} %get-tuple-element.157, f32[16,128]{1,0:T(8,128)S(1)} %bitcast.101, f32[16,128]{1,0:T(8,128)S(1)} %bitcast.103, f32[16,128]{1,0:T(8,128)S(1)} %bitcast.99, f32[16,256]{1,0:T(8,128)S(1)} %get-tuple-element.149, f32[16,256]{1,0:T(8,128)S(1)} %get-tuple-element.150, ...), kind=kOutput, calls=%fused_computation.4.clone.1 | convolution fusion | flops 818413568 | bytes 1196032 | tf_op jit(solution)/shard_map/while/body/eval_jaxpr/gqk,gqj->gkj/dot_general | solution.py:76
  217.0 5.5 %fusion.68 = f32[16,128,128]{2,1,0:T(8,128)S(1)} fusion(f32[16,256]{1,0:T(8,128)S(1)} %get-tuple-element.156, f32[16,128]{1,0:T(8,128)S(1)} %bitcast.94, f32[16,256]{1,0:T(8,128)S(1)} %get-tuple-element.149, f32[16,128]{1,0:T(8,128)S(1)} %bitcast.97, f32[16,256]{1,0:T(8,128)S(1)} %get-tuple-element.150, f32[16,128]{1,0:T(8,128)S(1)} %bitcast.91, ...), kind=kOutput, calls=%fused_computation.6.clone.1 | convolution fusion | flops 818413568 | bytes 1155072 | tf_op jit(solution)/shard_map/while/body/eval_jaxpr/gqk,gqj->gkj/dot_general | solution.py:75
  229.9 5.5 %fusion.70 = f32[16,128,128]{2,1,0:T(8,128)S(1)} fusion(f32[16,256]{1,0:T(8,128)S(1)} %get-tuple-element.157, f32[16,128]{1,0:T(8,128)S(1)} %bitcast.101, f32[16,128]{1,0:T(8,128)S(1)} %bitcast.103, f32[16,128]{1,0:T(8,128)S(1)} %bitcast.99, f32[16,256]{1,0:T(8,128)S(1)} %get-tuple-element.149, f32[16,256]{1,0:T(8,128)S(1)} %get-tuple-element.150, ...), kind=kOutput, calls=%fused_computation.4.clone.1 | convolution fusion | flops 818413568 | bytes 1196032 | tf_op jit(solution)/shard_map/while/body/eval_jaxpr/gqk,gqj->gkj/dot_general | solution.py:76
  248.3 5.5 %fusion.70 = f32[16,128,128]{2,1,0:T(8,128)S(1)} fusion(f32[16,256]{1,0:T(8,128)S(1)} %get-tuple-element.157, f32[16,128]{1,0:T(8,128)S(1)} %bitcast.101, f32[16,128]{1,0:T(8,128)S(1)} %bitcast.103, f32[16,128]{1,0:T(8,128)S(1)} %bitcast.99, f32[16,256]{1,0:T(8,128)S(1)} %get-tuple-element.149, f32[16,256]{1,0:T(8,128)S(1)} %get-tuple-element.150, ...), kind=kOutput, calls=%fused_computation.4.clone.1 | convolution fusion | flops 818413568 | bytes 1196032 | tf_op jit(solution)/shard_map/while/body/eval_jaxpr/gqk,gqj->gkj/dot_general | solution.py:76
  266.6 5.5 %fusion.70 = f32[16,128,128]{2,1,0:T(8,128)S(1)} fusion(f32[16,256]{1,0:T(8,128)S(1)} %get-tuple-element.157, f32[16,128]{1,0:T(8,128)S(1)} %bitcast.101, f32[16,128]{1,0:T(8,128)S(1)} %bitcast.103, f32[16,128]{1,0:T(8,128)S(1)} %bitcast.99, f32[16,256]{1,0:T(8,128)S(1)} %get-tuple-element.149, f32[16,256]{1,0:T(8,128)S(1)} %get-tuple-element.150, ...), kind=kOutput, calls=%fused_computation.4.clone.1 | convolution fusion | flops 818413568 | bytes 1196032 | tf_op jit(solution)/shard_map/while/body/eval_jaxpr/gqk,gqj->gkj/dot_general | solution.py:76
  272.1 5.5 %fusion.68 = f32[16,128,128]{2,1,0:T(8,128)S(1)} fusion(f32[16,256]{1,0:T(8,128)S(1)} %get-tuple-element.156, f32[16,128]{1,0:T(8,128)S(1)} %bitcast.94, f32[16,256]{1,0:T(8,128)S(1)} %get-tuple-element.149, f32[16,128]{1,0:T(8,128)S(1)} %bitcast.97, f32[16,256]{1,0:T(8,128)S(1)} %get-tuple-element.150, f32[16,128]{1,0:T(8,128)S(1)} %bitcast.91, ...), kind=kOutput, calls=%fused_computation.6.clone.1 | convolution fusion | flops 818413568 | bytes 1155072 | tf_op jit(solution)/shard_map/while/body/eval_jaxpr/gqk,gqj->gkj/dot_general | solution.py:75
  285.0 5.5 %fusion.70 = f32[16,128,128]{2,1,0:T(8,128)S(1)} fusion(f32[16,256]{1,0:T(8,128)S(1)} %get-tuple-element.157, f32[16,128]{1,0:T(8,128)S(1)} %bitcast.101, f32[16,128]{1,0:T(8,128)S(1)} %bitcast.103, f32[16,128]{1,0:T(8,128)S(1)} %bitcast.99, f32[16,256]{1,0:T(8,128)S(1)} %get-tuple-element.149, f32[16,256]{1,0:T(8,128)S(1)} %get-tuple-element.150, ...), kind=kOutput, calls=%fused_computation.4.clone.1 | convolution fusion | flops 818413568 | bytes 1196032 | tf_op jit(solution)/shard_map/while/body/eval_jaxpr/gqk,gqj->gkj/dot_general | solution.py:76
  303.4 5.5 %fusion.70 = f32[16,128,128]{2,1,0:T(8,128)S(1)} fusion(f32[16,256]{1,0:T(8,128)S(1)} %get-tuple-element.157, f32[16,128]{1,0:T(8,128)S(1)} %bitcast.101, f32[16,128]{1,0:T(8,128)S(1)} %bitcast.103, f32[16,128]{1,0:T(8,128)S(1)} %bitcast.99, f32[16,256]{1,0:T(8,128)S(1)} %get-tuple-element.149, f32[16,256]{1,0:T(8,128)S(1)} %get-tuple-element.150, ...), kind=kOutput, calls=%fused_computation.4.clone.1 | convolution fusion | flops 818413568 | bytes 1196032 | tf_op jit(solution)/shard_map/while/body/eval_jaxpr/gqk,gqj->gkj/dot_general | solution.py:76
  321.7 5.5 %fusion.70 = f32[16,128,128]{2,1,0:T(8,128)S(1)} fusion(f32[16,256]{1,0:T(8,128)S(1)} %get-tuple-element.157, f32[16,128]{1,0:T(8,128)S(1)} %bitcast.101, f32[16,128]{1,0:T(8,128)S(1)} %bitcast.103, f32[16,128]{1,0:T(8,128)S(1)} %bitcast.99, f32[16,256]{1,0:T(8,128)S(1)} %get-tuple-element.149, f32[16,256]{1,0:T(8,128)S(1)} %get-tuple-element.150, ...), kind=kOutput, calls=%fused_computation.4.clone.1 | convolution fusion | flops 818413568 | bytes 1196032 | tf_op jit(solution)/shard_map/while/body/eval_jaxpr/gqk,gqj->gkj/dot_general | solution.py:76
  340.1 5.5 %fusion.70 = f32[16,128,128]{2,1,0:T(8,128)S(1)} fusion(f32[16,256]{1,0:T(8,128)S(1)} %get-tuple-element.157, f32[16,128]{1,0:T(8,128)S(1)} %bitcast.101, f32[16,128]{1,0:T(8,128)S(1)} %bitcast.103, f32[16,128]{1,0:T(8,128)S(1)} %bitcast.99, f32[16,256]{1,0:T(8,128)S(1)} %get-tuple-element.149, f32[16,256]{1,0:T(8,128)S(1)} %get-tuple-element.150, ...), kind=kOutput, calls=%fused_computation.4.clone.1 | convolution fusion | flops 818413568 | bytes 1196032 | tf_op jit(solution)/shard_map/while/body/eval_jaxpr/gqk,gqj->gkj/dot_general | solution.py:76
  358.5 5.5 %fusion.70 = f32[16,128,128]{2,1,0:T(8,128)S(1)} fusion(f32[16,256]{1,0:T(8,128)S(1)} %get-tuple-element.157, f32[16,128]{1,0:T(8,128)S(1)} %bitcast.101, f32[16,128]{1,0:T(8,128)S(1)} %bitcast.103, f32[16,128]{1,0:T(8,128)S(1)} %bitcast.99, f32[16,256]{1,0:T(8,128)S(1)} %get-tuple-element.149, f32[16,256]{1,0:T(8,128)S(1)} %get-tuple-element.150, ...), kind=kOutput, calls=%fused_computation.4.clone.1 | convolution fusion | flops 818413568 | bytes 1196032 | tf_op jit(solution)/shard_map/while/body/eval_jaxpr/gqk,gqj->gkj/dot_general | solution.py:76
  376.8 5.5 %fusion.70 = f32[16,128,128]{2,1,0:T(8,128)S(1)} fusion(f32[16,256]{1,0:T(8,128)S(1)} %get-tuple-element.157, f32[16,128]{1,0:T(8,128)S(1)} %bitcast.101, f32[16,128]{1,0:T(8,128)S(1)} %bitcast.103, f32[16,128]{1,0:T(8,128)S(1)} %bitcast.99, f32[16,256]{1,0:T(8,128)S(1)} %get-tuple-element.149, f32[16,256]{1,0:T(8,128)S(1)} %get-tuple-element.150, ...), kind=kOutput, calls=%fused_computation.4.clone.1 | convolution fusion | flops 818413568 | bytes 1196032 | tf_op jit(solution)/shard_map/while/body/eval_jaxpr/gqk,gqj->gkj/dot_general | solution.py:76
  395.2 5.5 %fusion.70 = f32[16,128,128]{2,1,0:T(8,128)S(1)} fusion(f32[16,256]{1,0:T(8,128)S(1)} %get-tuple-element.157, f32[16,128]{1,0:T(8,128)S(1)} %bitcast.101, f32[16,128]{1,0:T(8,128)S(1)} %bitcast.103, f32[16,128]{1,0:T(8,128)S(1)} %bitcast.99, f32[16,256]{1,0:T(8,128)S(1)} %get-tuple-element.149, f32[16,256]{1,0:T(8,128)S(1)} %get-tuple-element.150, ...), kind=kOutput, calls=%fused_computation.4.clone.1 | convolution fusion | flops 818413568 | bytes 1196032 | tf_op jit(solution)/shard_map/while/body/eval_jaxpr/gqk,gqj->gkj/dot_general | solution.py:76
  410.3 24.2 %all_to_all.15 = f32[32,16,3,128]{3,1,2,0:T(8,128)S(1)} all-to-all(f32[32,16,3,128]{3,1,2,0:T(8,128)S(1)} %fusion.29), channel_id=1, replica_groups=mesh['gx'=4,'gy'=8] {'gx','gy'}, dimensions={0} | all-to-all | bytes 1572864 | tf_op jit(solution)/shard_map/all_to_all | solution.py:93
  (209 shorter events, 223.5 us)
Async XLA Ops:
  2.9 14.6 %all-to-all-start = ((s32[32,16,2]{1,2,0:T(2,128)}), s32[32,16,2]{1,2,0:T(2,128)S(1)}, u32[]{:S(2)}, u32[]{:S(2)}) async-start(s32[32,16,2]{1,2,0:T(2,128)} %copy.42), calls=%async_computation | async-start | bytes 65536 | tf_op jit(solution)/shard_map/all_to_all | solution.py:42
  32.6 3.2 copy-start.1
  32.6 74.4 %all-to-all-start.1 = ((f32[32,16,2,6,128]{4,1,3,2,0:T(8,128)}), f32[32,16,2,6,128]{4,1,3,2,0:T(8,128)S(1)}, u32[]{:S(2)}, u32[]{:S(2)}) async-start(f32[32,16,2,6,128]{4,1,3,2,0:T(8,128)} %pad_maximum_fusion), calls=%async_computation.1 | async-start | bytes 6291456 | tf_op jit(solution)/shard_map/all_to_all | solution.py:55
  114.8 1.0 copy-start
where the time goes:
time: 438 us; the launch traced here: 436 us
  matrix products  234 us (53%)
  waiting for transfers between devices  74.2 us (17%)
  other arithmetic  48 us (11%)
  local copies, waits for them, and re-layouts  44.8 us (10%)
  blocking collectives  24.2 us (6%)
  starting transfers between devices  10.4 us (2%)
    dot_general x16, matrix products, one_group(): dense_mix = jnp.einsum('gqk,gqj->gkj', weighted, pri_shape, precision=hp)  88.1 us
    dot_general x16, matrix products, one_group(): dense_sec = jnp.einsum('gqk,gqj->gkj', weighted, sec_shape, precision=hp)  87.4 us
    all_to_all x1, waiting for transfers between devices, body(): lax.all_to_all(outgoing.reshape(devices, capacity, 2, 6, node_count), ('g...  70.2 us
    reduce_sum x16, other arithmetic, shape_values(): return kernel / jnp.sum(kernel, axis=-1, keepdims=True)  34 us
    dot_general x16, matrix products, one_group(): jnp.einsum('gkj,gcj->gck', dense_mix, pri_here[:, 3:], precision=hp)  28.2 us
    dot_general x16, matrix products, one_group(): jnp.einsum('gkj,gcj->gck', dense_sec, sec_here[:, 3:], precision=hp)  27.7 us
    squeeze x32, local copies, waits for them, and re-layouts, body(): lax.map(one_group, (qpoints.reshape(groups, seg_group, 3, quad_points), w...  26.8 us
    all_to_all x1, blocking collectives, body(): lax.all_to_all(parcels.reshape(devices, capacity, 3, node_count), ('gx',...  24.2 us
  transfers between devices with their start and end apart: 2, of which 2 were waited for; matrix products, arithmetic and copies ran while one was open for 1% of the time, Pallas kernels for 0%

commit v1 on v0

v1 whole, which is shorter than its diff:
```python
import functools
import jax
import jax.numpy as jnp
from jax import lax
from jax.experimental import pallas as pl
from jax.experimental.pallas import tpu as pltpu
from jax.sharding import PartitionSpec as P

GROUP = 8
UNROLL = 8


def routing(block_ids, blocks_dev, capacity, slot_count):
    owners = block_ids // blocks_dev
    local_ids = block_ids % blocks_dev
    positions = jnp.arange(block_ids.shape[0], dtype=jnp.int32)
    same_owner = (owners[:, None] == owners[None, :]) & (positions[:, None] > positions[None, :])
    ranks = jnp.sum(same_owner.astype(jnp.int32), axis=1)
    slot_ids = owners * capacity + ranks
    matches = slot_ids[:, None] == jnp.arange(slot_count, dtype=jnp.int32)[None, :]
    request = jnp.sum(jnp.where(matches, local_ids[:, None], 0), axis=0)
    return slot_ids, request


def exchange(x):
    return lax.all_to_all(x, ("gx", "gy"), split_axis=0, concat_axis=0, tiled=True)


def gather_kernel(sec_ids, pri_ids, table, out):
    width = table.shape[1]

    @pl.loop(0, out.shape[0])
    def _(i):
        for j in range(UNROLL):
            s = i * UNROLL + j
            out[i, j : j + 1, :width] = table[pl.ds(sec_ids[s], 1), :]
            out[i, j : j + 1, width:] = table[pl.ds(pri_ids[s], 1), :]


def gather_rows(sec_ids, pri_ids, table):
    rows, width = sec_ids.shape[0], table.shape[1]
    return pl.pallas_call(
        gather_kernel,
        out_shape=jax.ShapeDtypeStruct((rows // UNROLL, UNROLL, 2 * width), jnp.float32),
        in_specs=[
            pl.BlockSpec(memory_space=pltpu.SMEM),
            pl.BlockSpec(memory_space=pltpu.SMEM),
            pl.BlockSpec(memory_space=pltpu.VMEM),
        ],
        out_specs=pl.BlockSpec(memory_space=pltpu.VMEM),
        name="gather_rows",
    )(sec_ids, pri_ids, table).reshape(rows, 2 * width)


def rounded(x):
    return x.astype(jnp.bfloat16).astype(jnp.float32)


def stack_rows(rows, iota):
    out = jnp.zeros(iota.shape, jnp.float32)
    for i, row in rows:
        out = jnp.where(iota == i, row, out)
    return out


def coupling_kernel(sec_slots, pri_slots, nodes, feats, weights, parcels):
    n = nodes.shape[1] // 12
    step = pl.program_id(0)

    @pl.when(step == 0)
    def _():
        parcels[...] = jnp.zeros_like(parcels)

    iota2 = lax.broadcasted_iota(jnp.int32, (8, 2 * n), 0)
    iota1 = lax.broadcasted_iota(jnp.int32, (8, n), 0)
    iotaq = lax.broadcasted_iota(jnp.int32, (8, feats.shape[2]), 0)
    bf = jnp.bfloat16
    f32 = jnp.float32

    def disp_rows(row):
        u = [row[:, (3 + c) * n : (4 + c) * n] for c in range(3)]
        full = stack_rows([(i + 4 * h, u[i]) for h in range(2) for i in range(3)], iota1)
        full = jnp.where((iota1 == 3) | (iota1 == 7), 1.0, full)
        high = rounded(full)
        both = jnp.where(iota1 < 4, high, full - high).astype(bf)
        return jnp.concatenate([both, both], axis=1)

    for g in range(feats.shape[0]):
        seg = step * feats.shape[0] + g
        slot = sec_slots[seg]
        sec = nodes[pl.ds(slot, 1), : 6 * n]
        pri = nodes[pl.ds(pri_slots[seg], 1), 6 * n :]
        x = [
            jnp.concatenate([sec[:, c * n : (c + 1) * n], pri[:, c * n : (c + 1) * n]], axis=1)
            for c in range(3)
        ]
        square = 2.0 * (x[0] * x[0] + x[1] * x[1] + x[2] * x[2])
        full = stack_rows(
            [(0, -4.0 * x[0]), (1, -4.0 * x[1]), (2, -4.0 * x[2]), (3, square), (4, 1.0)], iota2
        )
        high = rounded(full)
        rest = full - high
        mid = rounded(rest)
        low = rest - mid
        left = jnp.concatenate([high, high, mid, high, low, mid], axis=0)
        left = left.T.astype(bf)
        denom = jnp.dot(left, feats[g], preferred_element_type=f32)
        kern = 1.0 / denom
        kh = kern.astype(bf)
        kl = (kern - kh.astype(f32)).astype(bf)
        p1 = jnp.concatenate([kh[:n], kl[:n]], axis=0)
        p2 = jnp.concatenate([kh[n:], kl[n:]], axis=0)
        a1 = jnp.dot(disp_rows(sec), p1, preferred_element_type=f32)
        a2 = jnp.dot(disp_rows(pri), p2, preferred_element_type=f32)
        t1 = a1 + pltpu.roll(a1, 4, 0)
        t2 = a2 + pltpu.roll(a2, 4, 0)
        r1 = 1.0 / t1[3:4]
        r2 = 1.0 / t2[3:4]
        gap = (t1 * r1 - t2 * r2) * (weights[g : g + 1] * r1)
        high = rounded(gap)
        gap = jnp.where(iotaq < 4, high, gap - high).astype(bf)
        c = lax.dot_general(gap, p1, (((1,), (1,)), ((), ())), preferred_element_type=f32)
        c = c[:, :n] + c[:, n:]
        c = c + pltpu.roll(c, 4, 0)
        parcels[slot] = c[:3]


def coupling(sec_slots, pri_slots, nodes, feats, weights):
    segs, depth, points = feats.shape
    slots, width = nodes.shape
    node_count = width // 12
    return pl.pallas_call(
        coupling_kernel,
        grid_spec=pltpu.PrefetchScalarGridSpec(
            num_scalar_prefetch=2,
            grid=(segs // GROUP,),
            in_specs=[
                pl.BlockSpec((slots, width), lambda i, *_: (0, 0)),
                pl.BlockSpec((GROUP, depth, points), lambda i, *_: (i, 0, 0)),
                pl.BlockSpec((GROUP, points), lambda i, *_: (i, 0)),
            ],
            out_specs=pl.BlockSpec((slots, 3, node_count), lambda i, *_: (0, 0, 0)),
        ),
        out_shape=jax.ShapeDtypeStruct((slots, 3, node_count), jnp.float32),
        name="coupling",
    )(sec_slots, pri_slots, nodes, feats, weights).reshape(slots, 3 * node_count)


def assemble_kernel(ids, incoming, gap):
    blocks, comps, n = gap.shape
    slots = incoming.shape[0]
    match = lax.broadcasted_iota(jnp.int32, (blocks, slots), 0) == ids[...]
    select = jnp.where(match, 1.0, 0.0).astype(jnp.bfloat16)
    for c in range(comps):
        x = incoming[:, c * n : (c + 1) * n]
        high = rounded(x)
        rest = x - high
        mid = rounded(rest)
        pieces = jnp.concatenate([high, mid, rest - mid], axis=1).astype(jnp.bfloat16)
        y = jnp.dot(select, pieces, preferred_element_type=jnp.float32)
        gap[:, c, :] = y[:, :n] + (y[:, n : 2 * n] + y[:, 2 * n :])


def assemble(ids, incoming, blocks, comps):
    n = incoming.shape[1] // comps
    return pl.pallas_call(
        assemble_kernel,
        out_shape=jax.ShapeDtypeStruct((blocks, comps, n), jnp.float32),
        in_specs=[pl.BlockSpec(memory_space=pltpu.VMEM)] * 2,
        out_specs=pl.BlockSpec(memory_space=pltpu.VMEM),
        name="assemble",
    )(ids[None, :], incoming)


def point_features(qpoints):
    square = 1.0 + 2.0 * jnp.sum(qpoints * qpoints, axis=1, keepdims=True)
    ones = jnp.ones_like(square)
    full = jnp.concatenate([qpoints, ones, square, jnp.zeros_like(qpoints)], axis=1)
    high = lax.reduce_precision(full, 8, 7)
    rest = full - high
    mid = lax.reduce_precision(rest, 8, 7)
    low = rest - mid
    return jnp.concatenate([high, mid, high, low, high, mid], axis=1).astype(jnp.bfloat16)


def body(node_coords, node_disp, qpoints, qweights, qcount, sec_block, pri_block):
    devices = lax.axis_size("gx") * lax.axis_size("gy")
    blocks_dev, comps, node_count = node_coords.shape
    seg_count = qpoints.shape[0]
    quad_points = qpoints.shape[2]
    slot_count = 2 * seg_count
    capacity = slot_count // devices
    sec_slots, sec_request = routing(sec_block, blocks_dev, capacity, slot_count)
    pri_slots, pri_request = routing(pri_block, blocks_dev, capacity, slot_count)
    requests = jnp.stack(
        [sec_request.reshape(devices, capacity), pri_request.reshape(devices, capacity)], axis=1
    )
    received = exchange(requests)
    sec_ids = received[:, 0].reshape(slot_count)
    pri_ids = received[:, 1].reshape(slot_count)
    table = jnp.concatenate(
        [node_coords.reshape(blocks_dev, -1), node_disp.reshape(blocks_dev, -1)], axis=1
    )
    nodes = exchange(gather_rows(sec_ids, pri_ids, table))
    live = jnp.arange(quad_points, dtype=jnp.int32)[None, :] < qcount[:, None]
    weights = jnp.where(live, qweights, jnp.zeros_like(qweights))
    parcels = coupling(sec_slots, pri_slots, nodes, point_features(qpoints), weights)
    return assemble(sec_ids, exchange(parcels), blocks_dev, comps)


def solution(mesh):
    placed = (
        P(("gx", "gy"), None, None),
        P(("gx", "gy"), None, None),
        P(("gx", "gy"), None, None),
        P(("gx", "gy"), None),
        P(("gx", "gy")),
        P(("gx", "gy")),
        P(("gx", "gy")),
    )
    return jax.shard_map(
        body, mesh=mesh, in_specs=placed, out_specs=P(("gx", "gy"), None, None), check_vma=False
    )
```

time: 438 us -> 202 us (0.46)
  matrix products: 234 us -> 0 us
  Pallas kernels: 0 us -> 77.1 us
  other arithmetic: 48 us -> 14.7 us
  local copies, waits for them, and re-layouts: 44.8 us -> 13.9 us
  blocking collectives: 24.2 us -> 0 us
  waiting for transfers between devices: 74.2 us -> 81.8 us
    dot_general x66 -> x0, matrix products: 234 us -> none  [the longest x16 88.1 us: one_group(): dense_mix = jnp.einsum('gqk,gqj->gkj', weighted, pri_shape, precision=hp)]
    pallas_call x0 -> x3, Pallas kernels: none -> 77.1 us  [the longest x1 68.6 us: coupling(): pl.pallas_call(coupling_kernel, grid_spec=pltpu.PrefetchScalarGridSpec(nu...]
    reduce_sum x16 -> x1, other arithmetic: 34 us -> 0.06 us  [point_features(): square = 1.0 + 2.0 * jnp.sum(qpoints * qpoints, axis=1, keepdims=True)]
    squeeze x33 -> x0, local copies, waits for them, and re-layouts: 28.4 us -> none  [the longest x32 26.8 us: body(): lax.map(one_group, (qpoints.reshape(groups, seg_group, 3, quad_points), w...]
    all_to_all x1 -> x0, blocking collectives: 24.2 us -> none  [body(): lax.all_to_all(parcels.reshape(devices, capacity, 3, node_count), ('gx',...]
    gather x4 -> x0, local copies, waits for them, and re-layouts: 8.85 us -> none  [the longest x1 2.74 us: body(): jnp.take(node_data, received[:, 0], axis=0)]
    unnamed x0 -> x5, other arithmetic: none -> 8.82 us
    select_n x8 -> x0, other arithmetic: 8.4 us -> none  [the longest x2 3.36 us: body(): jnp.take(node_data, received[:, 1], axis=0)]
  transfers between devices with their start and end apart: 2 -> 3, of which waited for: 2 -> 3; matrix products, arithmetic and copies ran while one was open for 1% -> 9% of each run, Pallas kernels for 0% -> 0%
where the time goes in v1:
time: 202 us
  waiting for transfers between devices  81.8 us (40%)
  Pallas kernels  77.1 us (38%)
  other arithmetic  14.7 us (7%)
  starting transfers between devices  14 us (7%)
  local copies, waits for them, and re-layouts  13.9 us (7%)
    all_to_all x3, waiting for transfers between devices, exchange(): lax.all_to_all(x, ('gx', 'gy'), split_axis=0, concat_axis=0, tiled=True)  81.8 us
    pallas_call x1, Pallas kernels, coupling(): pl.pallas_call(coupling_kernel, grid_spec=pltpu.PrefetchScalarGridSpec(nu...  68.6 us
    all_to_all x3, starting transfers between devices, exchange(): lax.all_to_all(x, ('gx', 'gy'), split_axis=0, concat_axis=0, tiled=True)  14 us
    unnamed x5, other arithmetic  8.82 us
    unnamed x19, local copies, waits for them, and re-layouts  5.89 us
    pallas_call x1, Pallas kernels, gather_rows(): pl.pallas_call(gather_kernel, out_shape=jax.ShapeDtypeStruct((rows // UNR...  5.61 us
  transfers between devices with their start and end apart: 3, of which 3 were waited for; matrix products, arithmetic and copies ran while one was open for 9% of the time, Pallas kernels for 0%

profile of v1, /device:TPU:0, one launch (start us, length us, event | category | flops | bytes accessed | tf_op | source)
XLA Modules:
  0.0 201.7 jit_solution(9089823002161050740)
XLA Ops:
  0.0 0.8 and_select_fusion.1
  3.0 7.3 %all-to-all-start = ((s32[32,2,16]{2,1,0:T(2,128)}), s32[32,2,16]{2,1,0:T(2,128)S(1)}, u32[]{:S(2)}, u32[]{:S(2)}) async-start(s32[32,2,16]{2,1,0:T(2,128)} %copy.25), calls=%async_computation | async-start | bytes 65536 | tf_op jit(solution)/shard_map/all_to_all | solution.py:26
  10.3 1.3 copy.26
  12.3 1.1 pad_maximum_fusion.table
  13.4 4.1 %all-to-all-done = s32[32,2,16]{2,1,0:T(2,128)S(1)} async-done(((s32[32,2,16]{2,1,0:T(2,128)}), s32[32,2,16]{2,1,0:T(2,128)S(1)}, u32[]{:S(2)}, u32[]{:S(2)}) %all-to-all-start) | async-done | bytes 4128 | tf_op jit(solution)/shard_map/all_to_all | solution.py:26
  19.0 5.6 %gather_rows.1 = f32[64,8,1536]{2,1,0:T(8,128)} custom-call(s32[512]{0:T(512)} %reshape_squeeze.6.sec_ids, s32[512]{0:T(512)} %reshape_squeeze.7.pri_ids, f32[384,768]{1,0:T(8,128)} %pad_maximum_fusion.table), custom_call_target="tpu_custom_call" | custom-call | tf_op jit(solution)/shard_map/gather_rows/pallas_call | solution.py:42
  24.6 2.8 %all-to-all-start.1 = ((f32[32,16,1536]{2,1,0:T(8,128)}), f32[32,16,1536]{2,1,0:T(8,128)S(1)}, u32[]{:S(2)}, u32[]{:S(2)}) async-start(f32[32,16,1536]{2,1,0:T(8,128)} %bitcast.7), calls=%async_computation.1 | async-start | bytes 6291456 | tf_op jit(solution)/shard_map/all_to_all | solution.py:26
  27.4 1.8 copy.30
  29.6 0.8 fusion.4.weights
  30.4 1.6 constant_dynamic-update-slice_fusion.4
  32.1 1.8 constant_dynamic-update-slice_fusion.3
  33.9 1.7 constant_dynamic-update-slice_fusion.2
  35.6 2.0 fusion.1
  37.6 1.7 constant_dynamic-update-slice_fusion.1
  39.3 1.8 constant_dynamic-update-slice_fusion.feats
  41.1 57.7 %all-to-all-done.1 = f32[32,16,1536]{2,1,0:T(8,128)S(1)} async-done(((f32[32,16,1536]{2,1,0:T(8,128)}), f32[32,16,1536]{2,1,0:T(8,128)S(1)}, u32[]{:S(2)}, u32[]{:S(2)}) %all-to-all-start.1) | async-done | bytes 3145760 | tf_op jit(solution)/shard_map/all_to_all | solution.py:26
  98.8 1.7 copy-done
  100.5 68.6 %coupling.1 = f32[512,3,128]{2,1,0:T(4,128)} custom-call(s32[256]{0:T(256)} %copy-done.6, s32[256]{0:T(256)} %copy-done.5, f32[512,1536]{1,0:T(8,128)} %bitcast.8, bf16[256,48,256]{2,1,0:T(8,128)(2,1)} %constant_dynamic-update-slice_fusion.feats, f32[256,256]{1,0:T(8,128)} %fusion.4.weights), custom_call_target="tpu_custom_call" | custom-call | tf_op jit(solution)/shard_map/coupling/pallas_call | solution.py:132
  169.1 2.3 %all_to_all.21 = f32[32,16,384]{2,1,0:T(8,128)} reshape(f32[512,3,128]{2,1,0:T(4,128)} %coupling.1) | data formatting | bytes 1572864 | tf_op jit(solution)/shard_map/all_to_all | solution.py:26
  171.4 3.9 %all-to-all-start.2 = ((f32[32,16,384]{2,1,0:T(8,128)}), f32[32,16,384]{2,1,0:T(8,128)S(1)}, u32[]{:S(2)}, u32[]{:S(2)}) async-start(f32[32,16,384]{2,1,0:T(8,128)} %all_to_all.21), calls=%async_computation.2 | async-start | bytes 1572864 | tf_op jit(solution)/shard_map/all_to_all | solution.py:26
  176.0 19.9 %all-to-all-done.2 = f32[32,16,384]{2,1,0:T(8,128)S(1)} async-done(((f32[32,16,384]{2,1,0:T(8,128)}), f32[32,16,384]{2,1,0:T(8,128)S(1)}, u32[]{:S(2)}, u32[]{:S(2)}) %all-to-all-start.2) | async-done | bytes 786464 | tf_op jit(solution)/shard_map/all_to_all | solution.py:26
  195.9 0.9 copy-done.2
  196.8 2.9 %assemble.1 = f32[384,3,128]{2,1,0:T(4,128)} custom-call(s32[1,512]{1,0:T(1,128)} %broadcast_in_dim_reshape_squeeze.3.ids, f32[512,384]{1,0:T(8,128)} %bitcast.9), custom_call_target="tpu_custom_call" | custom-call | tf_op jit(solution)/shard_map/assemble/pallas_call | solution.py:166
  199.7 2.0 copy.31
  (37 shorter events, 5.4 us)
Async XLA Ops:
  0.0 11.8 %copy-start.3 = (f32[384,3,128]{2,0,1:T(8,128)S(1)}, f32[384,3,128]{2,0,1:T(8,128)}, u32[]{:S(2)}) copy-start(f32[384,3,128]{2,0,1:T(8,128)} %param.8) | copy-start | bytes 1769476
  1.8 10.5 %copy-start.5 = (s32[256]{0:T(256)}, s32[256]{0:T(256)S(1)}, u32[]{:S(2)}) copy-start(s32[256]{0:T(256)S(1)} %get-tuple-element.12.pri_slots) | copy-start | bytes 3076
  1.8 10.5 %copy-start.6 = (s32[256]{0:T(256)}, s32[256]{0:T(256)S(1)}, u32[]{:S(2)}) copy-start(s32[256]{0:T(256)S(1)} %get-tuple-element.13.sec_slots) | copy-start | bytes 3076
  3.0 14.6 %all-to-all-start = ((s32[32,2,16]{2,1,0:T(2,128)}), s32[32,2,16]{2,1,0:T(2,128)S(1)}, u32[]{:S(2)}, u32[]{:S(2)}) async-start(s32[32,2,16]{2,1,0:T(2,128)} %copy.25), calls=%async_computation | async-start | bytes 65536 | tf_op jit(solution)/shard_map/all_to_all | solution.py:26
  24.6 74.2 %all-to-all-start.1 = ((f32[32,16,1536]{2,1,0:T(8,128)}), f32[32,16,1536]{2,1,0:T(8,128)S(1)}, u32[]{:S(2)}, u32[]{:S(2)}) async-start(f32[32,16,1536]{2,1,0:T(8,128)} %bitcast.7), calls=%async_computation.1 | async-start | bytes 6291456 | tf_op jit(solution)/shard_map/all_to_all | solution.py:26
  27.4 1.8 copy-start.1
  27.4 2.2 %copy-start.4 = (f32[256,256]{1,0:T(8,128)S(1)}, f32[256,256]{1,0:T(8,128)}, u32[]{:S(2)}) copy-start(f32[256,256]{1,0:T(8,128)} %param.10) | copy-start | bytes 786436
  27.4 2.2 %copy-start.7 = (s32[256]{0:T(256)S(1)}, s32[256]{0:T(256)}, u32[]{:S(2)}) copy-start(s32[256]{0:T(256)} %param.11) | copy-start | bytes 3076
  98.8 1.7 copy-start
  171.4 24.5 %all-to-all-start.2 = ((f32[32,16,384]{2,1,0:T(8,128)}), f32[32,16,384]{2,1,0:T(8,128)S(1)}, u32[]{:S(2)}, u32[]{:S(2)}) async-start(f32[32,16,384]{2,1,0:T(8,128)} %all_to_all.21), calls=%async_computation.2 | async-start | bytes 1572864 | tf_op jit(solution)/shard_map/all_to_all | solution.py:26
  195.9 0.9 copy-start.2

commit v2 on v1

v2 whole, which is shorter than its diff:
```python
import functools
import jax
import jax.numpy as jnp
from jax import lax
from jax.experimental import pallas as pl
from jax.experimental.pallas import tpu as pltpu
from jax.sharding import PartitionSpec as P

GROUP = 16
UNROLL = 8


def routing(block_ids, blocks_dev, capacity, slot_count):
    owners = block_ids // blocks_dev
    local_ids = block_ids % blocks_dev
    positions = jnp.arange(block_ids.shape[0], dtype=jnp.int32)
    same_owner = (owners[:, None] == owners[None, :]) & (positions[:, None] > positions[None, :])
    ranks = jnp.sum(same_owner.astype(jnp.int32), axis=1)
    slot_ids = owners * capacity + ranks
    matches = slot_ids[:, None] == jnp.arange(slot_count, dtype=jnp.int32)[None, :]
    request = jnp.sum(jnp.where(matches, local_ids[:, None], 0), axis=0)
    return slot_ids, request


def exchange(x):
    return lax.all_to_all(x, ("gx", "gy"), split_axis=0, concat_axis=0, tiled=True)


def gather_kernel(ids, coords, disp, out):
    comps, _, n = coords.shape

    @pl.loop(0, out.shape[0])
    def _(i):
        for j in range(UNROLL):
            b = ids[i * UNROLL + j]
            for c in range(comps):
                out[i, j : j + 1, c * n : (c + 1) * n] = coords[c, pl.ds(b, 1), :]
                k = comps + c
                out[i, j : j + 1, k * n : (k + 1) * n] = disp[c, pl.ds(b, 1), :]


def gather_rows(ids, coords, disp):
    rows, width = ids.shape[0], 2 * coords.shape[0] * coords.shape[2]
    return pl.pallas_call(
        gather_kernel,
        out_shape=jax.ShapeDtypeStruct((rows // UNROLL, UNROLL, width), jnp.float32),
        in_specs=[
            pl.BlockSpec(memory_space=pltpu.SMEM),
            pl.BlockSpec(memory_space=pltpu.VMEM),
            pl.BlockSpec(memory_space=pltpu.VMEM),
        ],
        out_specs=pl.BlockSpec(memory_space=pltpu.VMEM),
        name="gather_rows",
    )(ids, coords, disp).reshape(rows, width)


def rounded(x):
    return x.astype(jnp.bfloat16).astype(jnp.float32)


def stack_rows(rows, iota):
    out = jnp.zeros(iota.shape, jnp.float32)
    for i, row in rows:
        out = jnp.where(iota == i, row, out)
    return out


def disp_rows(row, n):
    iota = lax.broadcasted_iota(jnp.int32, (8, n), 0)
    u = [row[:, (3 + c) * n : (4 + c) * n] for c in range(3)]
    full = stack_rows([(i + 4 * h, u[i]) for h in range(2) for i in range(3)], iota)
    full = jnp.where((iota == 3) | (iota == 7), 1.0, full)
    both = jnp.where(iota < 4, rounded(full), full - rounded(full)).astype(jnp.bfloat16)
    return jnp.concatenate([both, both], axis=1)


def side(row, feat, n):
    bf, f32 = jnp.bfloat16, jnp.float32
    iota = lax.broadcasted_iota(jnp.int32, (8, n), 0)
    x = [row[:, c * n : (c + 1) * n] for c in range(3)]
    square = 2.0 * (x[0] * x[0] + x[1] * x[1] + x[2] * x[2])
    full = stack_rows(
        [(0, -4.0 * x[0]), (1, -4.0 * x[1]), (2, -4.0 * x[2]), (3, square), (4, 1.0)], iota
    )
    high = rounded(full)
    rest = full - high
    mid = rounded(rest)
    left = jnp.concatenate([high, high, mid, high, rest - mid, mid], axis=0)
    kern = 1.0 / jnp.dot(left.T.astype(bf), feat, preferred_element_type=f32)
    kh = kern.astype(bf)
    kl = (kern - kh.astype(f32)).astype(bf)
    both = jnp.concatenate([kh, kl], axis=0)
    a = jnp.dot(disp_rows(row, n), both, preferred_element_type=f32)
    total = a + pltpu.roll(a, 4, 0)
    inv = 1.0 / total[3:4]
    return both, total * inv, inv


def pri_kernel(slots, nodes, feats, means):
    n = nodes.shape[1] // 6
    for g in range(feats.shape[0]):
        row = nodes[pl.ds(slots[pl.program_id(0) * feats.shape[0] + g], 1), :]
        means[g] = side(row, feats[g], n)[1]


def sec_kernel(slots, nodes, feats, weights, means, parcels):
    n = nodes.shape[1] // 6
    step = pl.program_id(0)

    @pl.when(step == 0)
    def _():
        parcels[...] = jnp.zeros_like(parcels)

    iota = lax.broadcasted_iota(jnp.int32, (8, feats.shape[2]), 0)
    for g in range(feats.shape[0]):
        slot = slots[step * feats.shape[0] + g]
        both, mean, inv = side(nodes[pl.ds(slot, 1), :], feats[g], n)
        gap = (mean - means[g]) * (weights[g : g + 1] * inv)
        high = rounded(gap)
        gap = jnp.where(iota < 4, high, gap - high).astype(jnp.bfloat16)
        c = lax.dot_general(
            gap, both, (((1,), (1,)), ((), ())), preferred_element_type=jnp.float32
        )
        c = c[:, :n] + c[:, n:]
        c = c + pltpu.roll(c, 4, 0)
        parcels[slot] = c[:3]


def cost(segs, points, n):
    return pl.CostEstimate(
        flops=8 * segs * points * n * 16, bytes_accessed=segs * points * 128, transcendentals=0
    )


def pri_means(slots_of, nodes, feats):
    segs, depth, points = feats.shape
    slots, width = nodes.shape
    return pl.pallas_call(
        pri_kernel,
        grid_spec=pltpu.PrefetchScalarGridSpec(
            num_scalar_prefetch=1,
            grid=(segs // GROUP,),
            in_specs=[
                pl.BlockSpec((slots, width), lambda i, *_: (0, 0)),
                pl.BlockSpec((GROUP, depth, points), lambda i, *_: (i, 0, 0)),
            ],
            out_specs=pl.BlockSpec((GROUP, 8, points), lambda i, *_: (i, 0, 0)),
        ),
        out_shape=jax.ShapeDtypeStruct((segs, 8, points), jnp.float32),
        cost_estimate=cost(segs, points, width // 6),
        name="pri_means",
    )(slots_of, nodes, feats)


def coupling(slots_of, nodes, feats, weights, means):
    segs, depth, points = feats.shape
    slots, width = nodes.shape
    n = width // 6
    return pl.pallas_call(
        sec_kernel,
        grid_spec=pltpu.PrefetchScalarGridSpec(
            num_scalar_prefetch=1,
            grid=(segs // GROUP,),
            in_specs=[
                pl.BlockSpec((slots, width), lambda i, *_: (0, 0)),
                pl.BlockSpec((GROUP, depth, points), lambda i, *_: (i, 0, 0)),
                pl.BlockSpec((GROUP, points), lambda i, *_: (i, 0)),
                pl.BlockSpec((GROUP, 8, points), lambda i, *_: (i, 0, 0)),
            ],
            out_specs=pl.BlockSpec((slots, 3, n), lambda i, *_: (0, 0, 0)),
        ),
        out_shape=jax.ShapeDtypeStruct((slots, 3, n), jnp.float32),
        cost_estimate=cost(segs, points, n),
        name="coupling",
    )(slots_of, nodes, feats, weights, means).reshape(slots, 3 * n)


def assemble_kernel(ids, incoming, gap):
    comps, blocks, n = gap.shape
    slots = incoming.shape[0]
    match = lax.broadcasted_iota(jnp.int32, (blocks, slots), 0) == ids[...]
    select = jnp.where(match, 1.0, 0.0).astype(jnp.bfloat16)
    for c in range(comps):
        x = incoming[:, c * n : (c + 1) * n]
        high = rounded(x)
        rest = x - high
        mid = rounded(rest)
        pieces = jnp.concatenate([high, mid, rest - mid], axis=1).astype(jnp.bfloat16)
        y = jnp.dot(select, pieces, preferred_element_type=jnp.float32)
        gap[c] = y[:, :n] + (y[:, n : 2 * n] + y[:, 2 * n :])


def assemble(ids, incoming, blocks, comps):
    n = incoming.shape[1] // comps
    return pl.pallas_call(
        assemble_kernel,
        out_shape=jax.ShapeDtypeStruct((comps, blocks, n), jnp.float32),
        in_specs=[pl.BlockSpec(memory_space=pltpu.VMEM)] * 2,
        out_specs=pl.BlockSpec(memory_space=pltpu.VMEM),
        name="assemble",
    )(ids[None, :], incoming).transpose(1, 0, 2)


def point_features(qpoints):
    square = 1.0 + 2.0 * jnp.sum(qpoints * qpoints, axis=1, keepdims=True)
    ones = jnp.ones_like(square)
    full = jnp.concatenate([qpoints, ones, square, jnp.zeros_like(qpoints)], axis=1)
    high = lax.reduce_precision(full, 8, 7)
    rest = full - high
    mid = lax.reduce_precision(rest, 8, 7)
    low = rest - mid
    return jnp.concatenate([high, mid, high, low, high, mid], axis=1).astype(jnp.bfloat16)


def body(node_coords, node_disp, qpoints, qweights, qcount, sec_block, pri_block):
    devices = lax.axis_size("gx") * lax.axis_size("gy")
    blocks_dev, comps, node_count = node_coords.shape
    seg_count = qpoints.shape[0]
    quad_points = qpoints.shape[2]
    slot_count = 2 * seg_count
    capacity = slot_count // devices
    sec_slots, sec_request = routing(sec_block, blocks_dev, capacity, slot_count)
    pri_slots, pri_request = routing(pri_block, blocks_dev, capacity, slot_count)
    requests = jnp.stack(
        [sec_request.reshape(devices, capacity), pri_request.reshape(devices, capacity)], axis=1
    )
    received = exchange(requests)
    sec_ids = received[:, 0].reshape(slot_count)
    pri_ids = received[:, 1].reshape(slot_count)
    coords = node_coords.transpose(1, 0, 2)
    disp = node_disp.transpose(1, 0, 2)
    pri_nodes = exchange(gather_rows(pri_ids, coords, disp))
    sec_rows, feats, pri_nodes = lax.optimization_barrier(
        (gather_rows(sec_ids, coords, disp), point_features(qpoints), pri_nodes)
    )
    sec_nodes = exchange(sec_rows)
    live = jnp.arange(quad_points, dtype=jnp.int32)[None, :] < qcount[:, None]
    weights = jnp.where(live, qweights, jnp.zeros_like(qweights))
    means = pri_means(pri_slots, pri_nodes, feats)
    parcels = coupling(sec_slots, sec_nodes, feats, weights, means)
    return assemble(sec_ids, exchange(parcels), blocks_dev, comps)


def solution(mesh):
    placed = (
        P(("gx", "gy"), None, None),
        P(("gx", "gy"), None, None),
        P(("gx", "gy"), None, None),
        P(("gx", "gy"), None),
        P(("gx", "gy")),
        P(("gx", "gy")),
        P(("gx", "gy")),
    )
    return jax.shard_map(
        body, mesh=mesh, in_specs=placed, out_specs=P(("gx", "gy"), None, None), check_vma=False
    )
```

time: 202 us -> 187 us (0.926)
  waiting for transfers between devices: 81.8 us -> 62.9 us
  blocking collectives: 0 us -> 14.4 us
  other arithmetic: 14.7 us -> 7.29 us
  starting transfers between devices: 14 us -> 10.2 us
  local copies, waits for them, and re-layouts: 13.9 us -> 10.3 us
  Pallas kernels: 77.1 us -> 80.6 us
    all_to_all x3, waiting for transfers between devices: 81.8 us -> 62.9 us  [exchange(): lax.all_to_all(x, ('gx', 'gy'), split_axis=0, concat_axis=0, tiled=True)]
    all_to_all x0 -> x1, blocking collectives: none -> 14.4 us  [exchange(): lax.all_to_all(x, ('gx', 'gy'), split_axis=0, concat_axis=0, tiled=True)]
    unnamed x5, other arithmetic: 8.82 us -> 3.55 us
    all_to_all x3, starting transfers between devices: 14 us -> 10.2 us  [exchange(): lax.all_to_all(x, ('gx', 'gy'), split_axis=0, concat_axis=0, tiled=True)]
    pallas_call x1 -> x2, Pallas kernels: 5.61 us -> 8.79 us  [gather_rows(): pl.pallas_call(gather_kernel, out_shape=jax.ShapeDtypeStruct((rows // UNR...]
    pallas_call x2 -> x3, Pallas kernels: 71.5 us -> 71.8 us  [the longest x1 50.6 us: coupling(): pl.pallas_call(sec_kernel, grid_spec=pltpu.PrefetchScalarGridSpec(num_sca...]
  transfers between devices with their start and end apart: 3 -> 3, of which waited for: 3 -> 3; matrix products, arithmetic and copies ran while one was open for 9% -> 4% of each run, Pallas kernels for 0% -> 12%
where the time goes in v2:
time: 187 us; the launch traced here: 186 us
  Pallas kernels  80.6 us (43%)
  waiting for transfers between devices  62.9 us (34%)
  blocking collectives  14.4 us (8%)
  local copies, waits for them, and re-layouts  10.3 us (6%)
  starting transfers between devices  10.2 us (5%)
  other arithmetic  7.29 us (4%)
    all_to_all x3, waiting for transfers between devices, exchange(): lax.all_to_all(x, ('gx', 'gy'), split_axis=0, concat_axis=0, tiled=True)  62.9 us
    pallas_call x1, Pallas kernels, coupling(): pl.pallas_call(sec_kernel, grid_spec=pltpu.PrefetchScalarGridSpec(num_sca...  50.6 us
    pallas_call x1, Pallas kernels, pri_means(): pl.pallas_call(pri_kernel, grid_spec=pltpu.PrefetchScalarGridSpec(num_sca...  18.5 us
    all_to_all x1, blocking collectives, exchange(): lax.all_to_all(x, ('gx', 'gy'), split_axis=0, concat_axis=0, tiled=True)  14.4 us
    all_to_all x3, starting transfers between devices, exchange(): lax.all_to_all(x, ('gx', 'gy'), split_axis=0, concat_axis=0, tiled=True)  10.2 us
    pallas_call x2, Pallas kernels, gather_rows(): pl.pallas_call(gather_kernel, out_shape=jax.ShapeDtypeStruct((rows // UNR...  8.79 us
    unnamed x19, local copies, waits for them, and re-layouts  5.33 us
  transfers between devices with their start and end apart: 3, of which 3 were waited for; matrix products, arithmetic and copies ran while one was open for 4% of the time, Pallas kernels for 12%

profile of v2, /device:TPU:0, one launch (start us, length us, event | category | flops | bytes accessed | tf_op | source)
XLA Modules:
  0.0 185.8 jit_solution(9809599998579340718)
XLA Ops:
  0.0 0.7 and_select_fusion.3
  1.1 0.7 and_select_fusion.1
  2.3 14.4 %all_to_all.39 = s32[32,2,16]{2,1,0:T(2,128)S(1)} all-to-all(s32[32,2,16]{2,1,0:T(2,128)S(1)} %copy.12), channel_id=1, replica_groups=mesh['gx'=4,'gy'=8] {'gx','gy'}, dimensions={0} | all-to-all | bytes 8192 | tf_op jit(solution)/shard_map/all_to_all | solution.py:26
  16.8 0.7 reshape_squeeze.7.ids
  17.4 4.3 %gather_rows.3 = f32[64,8,768]{2,1,0:T(8,128)} custom-call(s32[512]{0:T(512)} %reshape_squeeze.7.ids, f32[3,384,128]{2,1,0:T(8,128)} %bitcast.16, f32[3,384,128]{2,1,0:T(8,128)} %bitcast.18), custom_call_target="tpu_custom_call" | custom-call | tf_op jit(solution)/shard_map/gather_rows/pallas_call | solution.py:44
  21.8 2.8 %all-to-all-start.1 = ((f32[32,16,768]{2,1,0:T(8,128)}), f32[32,16,768]{2,1,0:T(8,128)S(1)}, u32[]{:S(2)}, u32[]{:S(2)}) async-start(f32[32,16,768]{2,1,0:T(8,128)} %bitcast.12), calls=%async_computation.1 | async-start | bytes 3145728 | tf_op jit(solution)/shard_map/all_to_all | solution.py:26
  26.2 0.8 constant_dynamic-update-slice_fusion.3
  27.7 0.9 fusion.1
  29.2 0.8 constant_dynamic-update-slice_fusion.feats
  30.0 2.7 %copy-done = bf16[256,48,256]{2,1,0:T(8,128)(2,1)} copy-done((bf16[256,48,256]{2,1,0:T(8,128)(2,1)}, bf16[256,48,256]{2,1,0:T(8,128)(2,1)S(1)}, u32[]{:S(2)}) %copy-start) | copy-done | bytes 6291480
  33.3 4.4 %gather_rows.2 = f32[64,8,768]{2,1,0:T(8,128)} custom-call(s32[512]{0:T(512)} %reshape_squeeze.6.ids, f32[3,384,128]{2,1,0:T(8,128)} %bitcast.17, f32[3,384,128]{2,1,0:T(8,128)} %bitcast.19), custom_call_target="tpu_custom_call" | custom-call | tf_op jit(solution)/shard_map/gather_rows/pallas_call | solution.py:44
  37.8 24.6 %all-to-all-done.1 = f32[32,16,768]{2,1,0:T(8,128)S(1)} async-done(((f32[32,16,768]{2,1,0:T(8,128)}), f32[32,16,768]{2,1,0:T(8,128)S(1)}, u32[]{:S(2)}, u32[]{:S(2)}) %all-to-all-start.1) | async-done | bytes 1572896 | tf_op jit(solution)/shard_map/all_to_all | solution.py:26
  62.4 3.6 %all-to-all-start.2 = ((f32[32,16,768]{2,1,0:T(8,128)}), f32[32,16,768]{2,1,0:T(8,128)S(1)}, u32[]{:S(2)}, u32[]{:S(2)}) async-start(f32[32,16,768]{2,1,0:T(8,128)} %bitcast.13), calls=%async_computation.2 | async-start | bytes 3145728 | tf_op jit(solution)/shard_map/all_to_all | solution.py:26
  66.0 0.8 fusion.4.weights
  66.8 18.5 %pri_means.1.means = f32[256,8,256]{2,1,0:T(8,128)} custom-call(s32[256]{0:T(256)} %copy-done.7, f32[512,768]{1,0:T(8,128)} %bitcast.11, bf16[256,48,256]{2,1,0:T(8,128)(2,1)} %copy-done), custom_call_target="tpu_custom_call" | custom-call | flops 1073741824 | bytes 8388608 | tf_op jit(solution)/shard_map/pri_means/pallas_call | solution.py:138
  85.3 18.3 %all-to-all-done.2 = f32[32,16,768]{2,1,0:T(8,128)S(1)} async-done(((f32[32,16,768]{2,1,0:T(8,128)}), f32[32,16,768]{2,1,0:T(8,128)S(1)}, u32[]{:S(2)}, u32[]{:S(2)}) %all-to-all-start.2) | async-done | bytes 1572896 | tf_op jit(solution)/shard_map/all_to_all | solution.py:26
  103.6 1.2 copy-done.2
  104.9 50.6 %coupling.1 = f32[512,3,128]{2,1,0:T(4,128)} custom-call(s32[256]{0:T(256)} %copy-done.6, f32[512,768]{1,0:T(8,128)} %bitcast.14, bf16[256,48,256]{2,1,0:T(8,128)(2,1)} %copy-done, f32[256,256]{1,0:T(8,128)} %fusion.4.weights, f32[256,8,256]{2,1,0:T(8,128)} %pri_means.1.means), custom_call_target="tpu_custom_call" | custom-call | flops 1073741824 | bytes 8388608 | tf_op jit(solution)/shard_map/coupling/pallas_call | solution.py:159
  155.4 2.3 %all_to_all.32 = f32[32,16,384]{2,1,0:T(8,128)} reshape(f32[512,3,128]{2,1,0:T(4,128)} %coupling.1) | data formatting | bytes 1572864 | tf_op jit(solution)/shard_map/all_to_all | solution.py:26
  157.8 3.8 %all-to-all-start.3 = ((f32[32,16,384]{2,1,0:T(8,128)}), f32[32,16,384]{2,1,0:T(8,128)S(1)}, u32[]{:S(2)}, u32[]{:S(2)}) async-start(f32[32,16,384]{2,1,0:T(8,128)} %all_to_all.32), calls=%async_computation.3 | async-start | bytes 1572864 | tf_op jit(solution)/shard_map/all_to_all | solution.py:26
  161.6 0.7 broadcast_in_dim_reshape_squeeze.3.ids
  162.2 19.9 %all-to-all-done.3 = f32[32,16,384]{2,1,0:T(8,128)S(1)} async-done(((f32[32,16,384]{2,1,0:T(8,128)}), f32[32,16,384]{2,1,0:T(8,128)S(1)}, u32[]{:S(2)}, u32[]{:S(2)}) %all-to-all-start.3) | async-done | bytes 786464 | tf_op jit(solution)/shard_map/all_to_all | solution.py:26
  182.2 0.9 copy-done.4
  183.0 2.7 %assemble.1 = f32[3,384,128]{2,1,0:T(8,128)} custom-call(s32[1,512]{1,0:T(1,128)} %broadcast_in_dim_reshape_squeeze.3.ids, f32[512,384]{1,0:T(8,128)} %bitcast.15), custom_call_target="tpu_custom_call" | custom-call | tf_op jit(solution)/shard_map/assemble/pallas_call | solution.py:195
  (37 shorter events, 4.5 us)
Async XLA Ops:
  0.9 20.9 %copy-start.6 = (s32[256]{0:T(256)}, s32[256]{0:T(256)S(1)}, u32[]{:S(2)}) copy-start(s32[256]{0:T(256)S(1)} %multiply_add_fusion.2.slots) | copy-start | bytes 3076
  2.0 19.8 %copy-start.7 = (s32[256]{0:T(256)}, s32[256]{0:T(256)S(1)}, u32[]{:S(2)}) copy-start(s32[256]{0:T(256)S(1)} %multiply_add_fusion.1.slots) | copy-start | bytes 3076
  21.8 2.9 %copy-start.3 = (f32[256,3,256]{2,0,1:T(8,128)S(1)}, f32[256,3,256]{2,0,1:T(8,128)}, u32[]{:S(2)}) copy-start(f32[256,3,256]{2,0,1:T(8,128)} %param.9) | copy-start | bytes 2359300
  21.8 40.6 %all-to-all-start.1 = ((f32[32,16,768]{2,1,0:T(8,128)}), f32[32,16,768]{2,1,0:T(8,128)S(1)}, u32[]{:S(2)}, u32[]{:S(2)}) async-start(f32[32,16,768]{2,1,0:T(8,128)} %bitcast.12), calls=%async_computation.1 | async-start | bytes 3145728 | tf_op jit(solution)/shard_map/all_to_all | solution.py:26
  30.0 2.7 %copy-start = (bf16[256,48,256]{2,1,0:T(8,128)(2,1)}, bf16[256,48,256]{2,1,0:T(8,128)(2,1)S(1)}, u32[]{:S(2)}) copy-start(bf16[256,48,256]{2,1,0:T(8,128)(2,1)S(1)} %constant_dynamic-update-slice_fusion.feats) | copy-start | bytes 18874372
  37.8 28.2 %copy-start.5 = (f32[256,256]{1,0:T(8,128)S(1)}, f32[256,256]{1,0:T(8,128)}, u32[]{:S(2)}) copy-start(f32[256,256]{1,0:T(8,128)} %param.10) | copy-start | bytes 786436
  37.8 28.2 %copy-start.8 = (s32[256]{0:T(256)S(1)}, s32[256]{0:T(256)}, u32[]{:S(2)}) copy-start(s32[256]{0:T(256)} %param.11) | copy-start | bytes 3076
  62.4 4.4 %copy-start.1 = (f32[32,16,768]{2,1,0:T(8,128)}, f32[32,16,768]{2,1,0:T(8,128)S(1)}, u32[]{:S(2)}) copy-start(f32[32,16,768]{2,1,0:T(8,128)S(1)} %all-to-all-done.1) | copy-start | bytes 4718596
  62.4 41.2 %all-to-all-start.2 = ((f32[32,16,768]{2,1,0:T(8,128)}), f32[32,16,768]{2,1,0:T(8,128)S(1)}, u32[]{:S(2)}, u32[]{:S(2)}) async-start(f32[32,16,768]{2,1,0:T(8,128)} %bitcast.13), calls=%async_computation.2 | async-start | bytes 3145728 | tf_op jit(solution)/shard_map/all_to_all | solution.py:26
  103.6 1.2 copy-start.2
  157.8 24.4 %all-to-all-start.3 = ((f32[32,16,384]{2,1,0:T(8,128)}), f32[32,16,384]{2,1,0:T(8,128)S(1)}, u32[]{:S(2)}, u32[]{:S(2)}) async-start(f32[32,16,384]{2,1,0:T(8,128)} %all_to_all.32), calls=%async_computation.3 | async-start | bytes 1572864 | tf_op jit(solution)/shard_map/all_to_all | solution.py:26
  182.2 0.9 copy-start.4

commit v3 on v2

--- a/solution.py
+++ b/solution.py
@@ -119,9 +119,9 @@
         high = rounded(gap)
         gap = jnp.where(iota < 4, high, gap - high).astype(jnp.bfloat16)
         c = lax.dot_general(
-            gap, both, (((1,), (1,)), ((), ())), preferred_element_type=jnp.float32
+            both, gap, (((1,), (1,)), ((), ())), preferred_element_type=jnp.float32
         )
-        c = c[:, :n] + c[:, n:]
+        c = (c[:n] + c[n:]).T
         c = c + pltpu.roll(c, 4, 0)
         parcels[slot] = c[:3]
 

time: 187 us -> 195 us (1.043)
  Pallas kernels: 80.6 us -> 88.5 us
    pallas_call x1, Pallas kernels: 50.6 us -> 58.5 us  [coupling(): pl.pallas_call(sec_kernel, grid_spec=pltpu.PrefetchScalarGridSpec(num_sca...]
where the time goes in v3:
time: 195 us; the launch traced here: 194 us
  Pallas kernels  88.5 us (45%)
  waiting for transfers between devices  62.9 us (32%)
  blocking collectives  14.4 us (7%)
  local copies, waits for them, and re-layouts  10.3 us (5%)
  starting transfers between devices  10.2 us (5%)
  other arithmetic  7.29 us (4%)
    all_to_all x3, waiting for transfers between devices, exchange(): lax.all_to_all(x, ('gx', 'gy'), split_axis=0, concat_axis=0, tiled=True)  62.9 us
    pallas_call x1, Pallas kernels, coupling(): pl.pallas_call(sec_kernel, grid_spec=pltpu.PrefetchScalarGridSpec(num_sca...  58.5 us
    pallas_call x1, Pallas kernels, pri_means(): pl.pallas_call(pri_kernel, grid_spec=pltpu.PrefetchScalarGridSpec(num_sca...  18.5 us
    all_to_all x1, blocking collectives, exchange(): lax.all_to_all(x, ('gx', 'gy'), split_axis=0, concat_axis=0, tiled=True)  14.4 us
    all_to_all x3, starting transfers between devices, exchange(): lax.all_to_all(x, ('gx', 'gy'), split_axis=0, concat_axis=0, tiled=True)  10.2 us
    pallas_call x2, Pallas kernels, gather_rows(): pl.pallas_call(gather_kernel, out_shape=jax.ShapeDtypeStruct((rows // UNR...  8.79 us
    unnamed x19, local copies, waits for them, and re-layouts  5.33 us
  transfers between devices with their start and end apart: 3, of which 3 were waited for; matrix products, arithmetic and copies ran while one was open for 4% of the time, Pallas kernels for 12%

profile of v3, /device:TPU:0, one launch (start us, length us, event | category | flops | bytes accessed | tf_op | source)
XLA Modules:
  0.0 193.7 jit_solution(3926654035721916244)
XLA Ops:
  0.0 0.7 and_select_fusion.3
  1.1 0.7 and_select_fusion.1
  2.3 14.4 %all_to_all.39 = s32[32,2,16]{2,1,0:T(2,128)S(1)} all-to-all(s32[32,2,16]{2,1,0:T(2,128)S(1)} %copy.12), channel_id=1, replica_groups=mesh['gx'=4,'gy'=8] {'gx','gy'}, dimensions={0} | all-to-all | bytes 8192 | tf_op jit(solution)/shard_map/all_to_all | solution.py:26
  16.8 0.7 reshape_squeeze.7.ids
  17.4 4.3 %gather_rows.3 = f32[64,8,768]{2,1,0:T(8,128)} custom-call(s32[512]{0:T(512)} %reshape_squeeze.7.ids, f32[3,384,128]{2,1,0:T(8,128)} %bitcast.16, f32[3,384,128]{2,1,0:T(8,128)} %bitcast.18), custom_call_target="tpu_custom_call" | custom-call | tf_op jit(solution)/shard_map/gather_rows/pallas_call | solution.py:44
  21.8 2.8 %all-to-all-start.1 = ((f32[32,16,768]{2,1,0:T(8,128)}), f32[32,16,768]{2,1,0:T(8,128)S(1)}, u32[]{:S(2)}, u32[]{:S(2)}) async-start(f32[32,16,768]{2,1,0:T(8,128)} %bitcast.12), calls=%async_computation.1 | async-start | bytes 3145728 | tf_op jit(solution)/shard_map/all_to_all | solution.py:26
  26.2 0.8 constant_dynamic-update-slice_fusion.3
  27.7 0.9 fusion.1
  29.2 0.8 constant_dynamic-update-slice_fusion.feats
  30.0 2.7 %copy-done = bf16[256,48,256]{2,1,0:T(8,128)(2,1)} copy-done((bf16[256,48,256]{2,1,0:T(8,128)(2,1)}, bf16[256,48,256]{2,1,0:T(8,128)(2,1)S(1)}, u32[]{:S(2)}) %copy-start) | copy-done | bytes 6291480
  33.3 4.4 %gather_rows.2 = f32[64,8,768]{2,1,0:T(8,128)} custom-call(s32[512]{0:T(512)} %reshape_squeeze.6.ids, f32[3,384,128]{2,1,0:T(8,128)} %bitcast.17, f32[3,384,128]{2,1,0:T(8,128)} %bitcast.19), custom_call_target="tpu_custom_call" | custom-call | tf_op jit(solution)/shard_map/gather_rows/pallas_call | solution.py:44
  37.8 24.6 %all-to-all-done.1 = f32[32,16,768]{2,1,0:T(8,128)S(1)} async-done(((f32[32,16,768]{2,1,0:T(8,128)}), f32[32,16,768]{2,1,0:T(8,128)S(1)}, u32[]{:S(2)}, u32[]{:S(2)}) %all-to-all-start.1) | async-done | bytes 1572896 | tf_op jit(solution)/shard_map/all_to_all | solution.py:26
  62.4 3.6 %all-to-all-start.2 = ((f32[32,16,768]{2,1,0:T(8,128)}), f32[32,16,768]{2,1,0:T(8,128)S(1)}, u32[]{:S(2)}, u32[]{:S(2)}) async-start(f32[32,16,768]{2,1,0:T(8,128)} %bitcast.13), calls=%async_computation.2 | async-start | bytes 3145728 | tf_op jit(solution)/shard_map/all_to_all | solution.py:26
  66.0 0.8 fusion.4.weights
  66.8 18.5 %pri_means.1.means = f32[256,8,256]{2,1,0:T(8,128)} custom-call(s32[256]{0:T(256)} %copy-done.7, f32[512,768]{1,0:T(8,128)} %bitcast.11, bf16[256,48,256]{2,1,0:T(8,128)(2,1)} %copy-done), custom_call_target="tpu_custom_call" | custom-call | flops 1073741824 | bytes 8388608 | tf_op jit(solution)/shard_map/pri_means/pallas_call | solution.py:138
  85.3 18.3 %all-to-all-done.2 = f32[32,16,768]{2,1,0:T(8,128)S(1)} async-done(((f32[32,16,768]{2,1,0:T(8,128)}), f32[32,16,768]{2,1,0:T(8,128)S(1)}, u32[]{:S(2)}, u32[]{:S(2)}) %all-to-all-start.2) | async-done | bytes 1572896 | tf_op jit(solution)/shard_map/all_to_all | solution.py:26
  103.6 1.2 copy-done.2
  104.9 58.5 %coupling.1 = f32[512,3,128]{2,1,0:T(4,128)} custom-call(s32[256]{0:T(256)} %copy-done.6, f32[512,768]{1,0:T(8,128)} %bitcast.14, bf16[256,48,256]{2,1,0:T(8,128)(2,1)} %copy-done, f32[256,256]{1,0:T(8,128)} %fusion.4.weights, f32[256,8,256]{2,1,0:T(8,128)} %pri_means.1.means), custom_call_target="tpu_custom_call" | custom-call | flops 1073741824 | bytes 8388608 | tf_op jit(solution)/shard_map/coupling/pallas_call | solution.py:159
  163.4 2.3 %all_to_all.32 = f32[32,16,384]{2,1,0:T(8,128)} reshape(f32[512,3,128]{2,1,0:T(4,128)} %coupling.1) | data formatting | bytes 1572864 | tf_op jit(solution)/shard_map/all_to_all | solution.py:26
  165.7 3.8 %all-to-all-start.3 = ((f32[32,16,384]{2,1,0:T(8,128)}), f32[32,16,384]{2,1,0:T(8,128)S(1)}, u32[]{:S(2)}, u32[]{:S(2)}) async-start(f32[32,16,384]{2,1,0:T(8,128)} %all_to_all.32), calls=%async_computation.3 | async-start | bytes 1572864 | tf_op jit(solution)/shard_map/all_to_all | solution.py:26
  169.5 0.7 broadcast_in_dim_reshape_squeeze.3.ids
  170.2 19.9 %all-to-all-done.3 = f32[32,16,384]{2,1,0:T(8,128)S(1)} async-done(((f32[32,16,384]{2,1,0:T(8,128)}), f32[32,16,384]{2,1,0:T(8,128)S(1)}, u32[]{:S(2)}, u32[]{:S(2)}) %all-to-all-start.3) | async-done | bytes 786464 | tf_op jit(solution)/shard_map/all_to_all | solution.py:26
  190.1 0.9 copy-done.4
  191.0 2.7 %assemble.1 = f32[3,384,128]{2,1,0:T(8,128)} custom-call(s32[1,512]{1,0:T(1,128)} %broadcast_in_dim_reshape_squeeze.3.ids, f32[512,384]{1,0:T(8,128)} %bitcast.15), custom_call_target="tpu_custom_call" | custom-call | tf_op jit(solution)/shard_map/assemble/pallas_call | solution.py:195
  (37 shorter events, 4.5 us)
Async XLA Ops:
  0.9 20.9 %copy-start.6 = (s32[256]{0:T(256)}, s32[256]{0:T(256)S(1)}, u32[]{:S(2)}) copy-start(s32[256]{0:T(256)S(1)} %multiply_add_fusion.2.slots) | copy-start | bytes 3076
  2.0 19.8 %copy-start.7 = (s32[256]{0:T(256)}, s32[256]{0:T(256)S(1)}, u32[]{:S(2)}) copy-start(s32[256]{0:T(256)S(1)} %multiply_add_fusion.1.slots) | copy-start | bytes 3076
  21.8 2.9 %copy-start.3 = (f32[256,3,256]{2,0,1:T(8,128)S(1)}, f32[256,3,256]{2,0,1:T(8,128)}, u32[]{:S(2)}) copy-start(f32[256,3,256]{2,0,1:T(8,128)} %param.9) | copy-start | bytes 2359300
  21.8 40.6 %all-to-all-start.1 = ((f32[32,16,768]{2,1,0:T(8,128)}), f32[32,16,768]{2,1,0:T(8,128)S(1)}, u32[]{:S(2)}, u32[]{:S(2)}) async-start(f32[32,16,768]{2,1,0:T(8,128)} %bitcast.12), calls=%async_computation.1 | async-start | bytes 3145728 | tf_op jit(solution)/shard_map/all_to_all | solution.py:26
  30.0 2.7 %copy-start = (bf16[256,48,256]{2,1,0:T(8,128)(2,1)}, bf16[256,48,256]{2,1,0:T(8,128)(2,1)S(1)}, u32[]{:S(2)}) copy-start(bf16[256,48,256]{2,1,0:T(8,128)(2,1)S(1)} %constant_dynamic-update-slice_fusion.feats) | copy-start | bytes 18874372
  37.8 28.2 %copy-start.5 = (f32[256,256]{1,0:T(8,128)S(1)}, f32[256,256]{1,0:T(8,128)}, u32[]{:S(2)}) copy-start(f32[256,256]{1,0:T(8,128)} %param.10) | copy-start | bytes 786436
  37.8 28.2 %copy-start.8 = (s32[256]{0:T(256)S(1)}, s32[256]{0:T(256)}, u32[]{:S(2)}) copy-start(s32[256]{0:T(256)} %param.11) | copy-start | bytes 3076
  62.4 4.4 %copy-start.1 = (f32[32,16,768]{2,1,0:T(8,128)}, f32[32,16,768]{2,1,0:T(8,128)S(1)}, u32[]{:S(2)}) copy-start(f32[32,16,768]{2,1,0:T(8,128)S(1)} %all-to-all-done.1) | copy-start | bytes 4718596
  62.4 41.2 %all-to-all-start.2 = ((f32[32,16,768]{2,1,0:T(8,128)}), f32[32,16,768]{2,1,0:T(8,128)S(1)}, u32[]{:S(2)}, u32[]{:S(2)}) async-start(f32[32,16,768]{2,1,0:T(8,128)} %bitcast.13), calls=%async_computation.2 | async-start | bytes 3145728 | tf_op jit(solution)/shard_map/all_to_all | solution.py:26
  103.6 1.2 copy-start.2
  165.7 24.4 %all-to-all-start.3 = ((f32[32,16,384]{2,1,0:T(8,128)}), f32[32,16,384]{2,1,0:T(8,128)S(1)}, u32[]{:S(2)}, u32[]{:S(2)}) async-start(f32[32,16,384]{2,1,0:T(8,128)} %all_to_all.32), calls=%async_computation.3 | async-start | bytes 1572864 | tf_op jit(solution)/shard_map/all_to_all | solution.py:26
  190.1 0.9 copy-start.4
